TPU v7x, 32 devices: a whole 2x2x4 slice. The times are simulated.
32 devices in a mesh: fsdp: 2 (over x), context: 4 (over z), tensor: 4 (over y, core).
Axes of the slice: x: 2, y: 2, z: 4, core: 2. Of those that a mesh axis runs over, the one named last changes fastest.
Arguments:
- activations: bfloat16 [2, 2048, 1152], P('fsdp', 'context'), may hold values from -6 to 6
- positions: int32 [2, 2048], P('fsdp', 'context'), may hold values from 0 to 2047, as said below
- seg_ids: int32 [2, 2048], P('fsdp', 'context'), may hold values from 0 to 3, as said below
- norm_gains: bfloat16 [4, 1152], P(None, ('fsdp', 'context')), may hold values from 0.5 to 1.5
- head_gains: bfloat16 [2, 256], P(None, ('fsdp', 'context')), may hold values from 0.25 to 1.75
- w_query: bfloat16 [1152, 1024], P(('fsdp', 'context'), 'tensor'), may hold values from -0.1875 to 0.1875
- w_keyval: bfloat16 [1152, 512], P(('fsdp', 'context')), may hold values from -0.1875 to 0.1875
- w_out: bfloat16 [1152, 1024], P(('fsdp', 'context'), 'tensor'), may hold values from -0.1875 to 0.1875
- w_gateup: bfloat16 [1152, 2, 6912], P(('fsdp', 'context'), None, 'tensor'), may hold values from -0.1875 to 0.1875
- w_down: bfloat16 [1152, 6912], P(('fsdp', 'context'), 'tensor'), may hold values from -0.078125 to 0.078125
- cotangent: bfloat16 [2, 2048, 1152], P('fsdp', 'context'), may hold values from -6 to 6
Outputs:
- block_output: bfloat16 [2, 2048, 1152], P('fsdp', 'context')
- input_grad: bfloat16 [2, 2048, 1152], P('fsdp', 'context')
- norm_gains_grad: float32 [4, 1152], P(None, ('fsdp', 'context'))
- head_gains_grad: float32 [2, 256], P(None, ('fsdp', 'context'))
- w_query_grad: float32 [1152, 1024], P(('fsdp', 'context'), 'tensor')
- w_keyval_grad: float32 [1152, 512], P(('fsdp', 'context'))
- w_out_grad: float32 [1152, 1024], P(('fsdp', 'context'), 'tensor')
- w_gateup_grad: float32 [1152, 2, 6912], P(('fsdp', 'context'), None, 'tensor')
- w_down_grad: float32 [1152, 6912], P(('fsdp', 'context'), 'tensor')
Inputs may be any that keep to these rules, and one draw needn't show every extreme that they name: `positions`: within a sequence, a document is a run of consecutive tokens with one document number; numbers never fall along a sequence. Positions are 0 at a document's first token and rise by one from token to token inside it. The first sequence is one document. `seg_ids`: document numbers of a sequence start at 0 and never fall along it.
All inputs are finite; a program needn't handle non-finite values.
Results may differ from a plain program's by a relative error of at most 0.024.
Values may be sent and summed in bfloat16 or wider, within the bound.
A program may use at most 192 MiB of HBM per device.

v0:
```python
import jax
import jax.numpy as jnp
from jax import lax
from jax.sharding import PartitionSpec as P

HD = 256
WINDOW = 512
EPSILON = 1e-06


def from_behind(block, axis, distance):
    devices = range(lax.axis_size(axis))
    route = [(i - distance, i) for i in devices if i - distance in devices]
    return lax.ppermute(block, axis, route)


def rms_norm(values, gain):
    factor = lax.rsqrt(jnp.mean(values * values, axis=-1, keepdims=True) + EPSILON)
    return values * factor * gain


def rotate(tensor, places):
    width_all = tensor.shape[-1]
    half_width = width_all // 2
    freqs = jnp.power(10000.0, -jnp.arange(half_width, dtype=jnp.float32) * 2.0 / width_all)
    angles = places.astype(jnp.float32)[:, None] * freqs[None, :]
    cosine = jnp.cos(angles)[:, None, :]
    sine = jnp.sin(angles)[:, None, :]
    first_half = tensor[..., :half_width]
    second_half = tensor[..., half_width:]
    return jnp.concatenate(
        [first_half * cosine - second_half * sine, second_half * cosine + first_half * sine],
        axis=-1,
    )


def glu(gate_up):
    return jax.nn.gelu(gate_up[:, 0], approximate=True) * gate_up[:, 1]


def contract_last(left_side, right_side):
    return lax.dot_general(
        left_side, right_side, (((1,), (1,)), ((), ())), preferred_element_type=jnp.float32
    )


def contract_first(left_side, right_side):
    return lax.dot_general(
        left_side, right_side, (((0,), (0,)), ((), ())), preferred_element_type=jnp.float32
    )


def shards(
    activations,
    positions,
    seg_ids,
    norm_gains,
    head_gains,
    w_query,
    w_keyval,
    w_out,
    w_gateup,
    w_down,
    cotangent,
):
    tokens = activations.shape[1]
    local_heads = w_query.shape[1] // HD
    inputs = activations[0].astype(jnp.float32)
    places = positions[0]
    documents = seg_ids[0]
    gains_all, heads_all, query_all, keyval_all, out_all = (
        lax.all_gather(norm_gains, ("fsdp", "context"), axis=1, tiled=True),
        lax.all_gather(head_gains, ("fsdp", "context"), axis=1, tiled=True),
        lax.all_gather(w_query, ("fsdp", "context"), axis=0, tiled=True),
        lax.all_gather(w_keyval, ("fsdp", "context"), axis=0, tiled=True),
        lax.all_gather(w_out, ("fsdp", "context"), axis=0, tiled=True),
    )
    gains_f = gains_all.astype(jnp.float32)
    heads_f = heads_all.astype(jnp.float32)
    normed_f, input_back = jax.vjp(rms_norm, inputs, gains_f[0])
    normed = normed_f.astype(jnp.bfloat16)
    query_raw = jnp.dot(normed, query_all, preferred_element_type=jnp.float32).reshape(
        tokens, local_heads, HD
    )
    keyval_raw = jnp.dot(normed, keyval_all, preferred_element_type=jnp.float32)

    def prepare(raw_heads, head_gain):
        return rotate(rms_norm(raw_heads, head_gain), places)

    query_rot, query_back = jax.vjp(prepare, query_raw, heads_f[0])
    key_rot, key_back = jax.vjp(prepare, keyval_raw[:, None, :HD], heads_f[1])
    queries = query_rot.astype(jnp.bfloat16)
    own_keyval = jnp.concatenate([key_rot[:, 0], keyval_raw[:, HD:]], axis=1).astype(jnp.bfloat16)
    labels = jnp.stack([places, documents])
    keep_from = tokens - tokens
    left_keyval, left_labels = from_behind((own_keyval, labels), "context", 1)
    keys_all = jnp.concatenate([left_keyval, own_keyval], axis=0)
    key_places = jnp.concatenate([left_labels[0], places])
    key_documents = jnp.concatenate([left_labels[1], documents])
    has_left = lax.axis_index("context") > 0
    key_live = jnp.concatenate([jnp.full((tokens,), has_left), jnp.ones((tokens,), dtype=bool)])
    scale_factor = HD ** (-0.5)
    block_rows = 512
    block_starts = jnp.arange(tokens // block_rows) * block_rows

    def block_scores():
        spacing = places[:, None] - key_places[None, :]
        visible = (
            key_live[None, :]
            & (documents[:, None] == key_documents[None, :])
            & (spacing >= 0)
            & (spacing < WINDOW)
        )
        raw_scores = (
            jnp.einsum("qhd,kd->hqk", queries, keys_all[:, :HD], preferred_element_type=jnp.float32)
            * scale_factor
        )
        return (jnp.where(visible[None], raw_scores, -1e30), keys_all, queries)

    def forward_block(start):
        scores, near_keyval, query_block = block_scores()
        row_top = jnp.max(scores, axis=-1, keepdims=True)
        raised = jnp.exp(scores - row_top)
        row_total = jnp.sum(raised, axis=-1, keepdims=True)
        probs = raised / row_total
        mixed_block = jnp.einsum(
            "hqk,kd->qhd",
            probs.astype(jnp.bfloat16),
            near_keyval[:, HD:],
            preferred_element_type=jnp.float32,
        )
        return (mixed_block.astype(jnp.bfloat16), row_top + jnp.log(row_total))

    mixed_blocks, log_blocks = lax.map(forward_block, block_starts)
    mixed_low = mixed_blocks.reshape(tokens, local_heads * HD)
    branch = lax.psum(contract_last(mixed_low, out_all).astype(jnp.bfloat16), "tensor").astype(
        jnp.float32
    )
    post_attn, post_attn_back = jax.vjp(rms_norm, branch, gains_f[1])
    hidden = inputs + post_attn
    normed_mlp_f, pre_mlp_back = jax.vjp(rms_norm, hidden, gains_f[2])
    normed_mlp = normed_mlp_f.astype(jnp.bfloat16)
    columns = normed_mlp
    gate_up = jnp.einsum(
        "bn,nkf->bkf",
        columns,
        lax.all_gather(w_gateup, ("fsdp", "context"), axis=0, tiled=True),
        preferred_element_type=jnp.float32,
    )
    active_f, glu_back = jax.vjp(glu, gate_up)
    active = active_f.astype(jnp.bfloat16)
    down = lax.psum(
        contract_last(
            active, lax.all_gather(w_down, ("fsdp", "context"), axis=0, tiled=True)
        ).astype(jnp.bfloat16),
        "tensor",
    ).astype(jnp.float32)
    post_mlp, post_mlp_back = jax.vjp(rms_norm, down, gains_f[3])
    result = hidden + post_mlp
    grad_out = cotangent[0].astype(jnp.float32)
    d_down, gain_post_mlp = post_mlp_back(grad_out)
    down_low = d_down.astype(jnp.bfloat16)
    columns = down_low
    d_active = jnp.dot(
        columns,
        lax.all_gather(w_down, ("fsdp", "context"), axis=0, tiled=True),
        preferred_element_type=jnp.float32,
    )
    d_gate_up = glu_back(d_active)[0].astype(jnp.bfloat16)
    d_normed_part = jnp.einsum(
        "bkf,nkf->bn",
        d_gate_up,
        lax.all_gather(w_gateup, ("fsdp", "context"), axis=0, tiled=True),
        preferred_element_type=jnp.float32,
    )
    d_normed_mlp = lax.psum(d_normed_part.astype(jnp.bfloat16), "tensor").astype(jnp.float32)
    d_hidden_norm, gain_pre_mlp = pre_mlp_back(d_normed_mlp)
    d_hidden = grad_out + d_hidden_norm
    features = normed_mlp
    grad_cols = down_low
    gate_up_term = jnp.einsum(
        "bn,bkf->nkf", features, d_gate_up, preferred_element_type=jnp.float32
    )
    down_term = contract_first(grad_cols, active)
    scatter = lambda part: lax.psum_scatter(
        part.astype(jnp.bfloat16), ("fsdp", "context"), scatter_dimension=0, tiled=True
    ).astype(jnp.float32)
    gate_grad = scatter(gate_up_term[:, 0])
    up_grad = scatter(gate_up_term[:, 1])
    down_grad = scatter(down_term)
    d_branch, gain_post_attn = post_attn_back(d_hidden)
    branch_low = d_branch.astype(jnp.bfloat16)
    d_mixed = jnp.dot(branch_low, out_all, preferred_element_type=jnp.float32)
    d_mixed_low = d_mixed.astype(jnp.bfloat16).reshape(tokens, local_heads, HD)

    def backward_block(carry, item):
        start, log_block = item
        scores, near_keyval, query_block = block_scores()
        probs_again = jnp.exp(scores - log_block)
        d_probs = jnp.einsum(
            "qhd,kd->hqk", d_mixed_low, near_keyval[:, HD:], preferred_element_type=jnp.float32
        )
        row_inner = jnp.sum(probs_again * d_probs, axis=-1, keepdims=True)
        d_scores = (probs_again * (d_probs - row_inner)).astype(jnp.bfloat16)
        d_query_block = (
            jnp.einsum(
                "hqk,kd->qhd", d_scores, near_keyval[:, :HD], preferred_element_type=jnp.float32
            )
            * scale_factor
        )
        d_keys = (
            jnp.einsum("hqk,qhd->kd", d_scores, query_block, preferred_element_type=jnp.float32)
            * scale_factor
        )
        d_values = jnp.einsum(
            "hqk,qhd->kd",
            probs_again.astype(jnp.bfloat16),
            d_mixed_low,
            preferred_element_type=jnp.float32,
        )
        updated = carry + jnp.concatenate([d_keys, d_values], axis=1)
        return (updated, d_query_block)

    d_keyval, d_query_blocks = lax.scan(
        backward_block,
        jnp.zeros((tokens + tokens, 2 * HD), jnp.float32),
        (block_starts, log_blocks),
    )
    d_queries = d_query_blocks.reshape(tokens, local_heads, HD)
    returned = from_behind(d_keyval[:tokens].astype(jnp.bfloat16), "context", -1).astype(
        jnp.float32
    )
    own_grad = d_keyval[tokens:].at[keep_from:].add(returned)
    d_query_raw, gain_query = query_back(d_queries)
    d_query_low = d_query_raw.reshape(tokens, local_heads * HD).astype(jnp.bfloat16)
    d_normed_query, keyval_grad, gain_query_all = (
        lax.psum(contract_last(d_query_low, query_all).astype(jnp.bfloat16), "tensor").astype(
            jnp.float32
        ),
        lax.psum(own_grad.astype(jnp.bfloat16), "tensor").astype(jnp.float32),
        lax.psum(gain_query.astype(jnp.bfloat16), "tensor").astype(jnp.float32),
    )
    d_key_raw, gain_key = key_back(keyval_grad[:, None, :HD])
    d_keyval_low = jnp.concatenate([d_key_raw[:, 0], keyval_grad[:, HD:]], axis=1).astype(
        jnp.bfloat16
    )
    d_normed = d_normed_query + contract_last(d_keyval_low, keyval_all)
    d_input_norm, gain_input = input_back(d_normed)
    input_total = d_hidden + d_input_norm
    features = normed
    grad_cols = branch_low
    attn_grads = lax.psum_scatter(
        jnp.stack(
            [contract_first(features, d_query_low), contract_first(grad_cols, mixed_low)], axis=1
        ).astype(jnp.bfloat16),
        ("fsdp", "context"),
        scatter_dimension=0,
        tiled=True,
    ).astype(jnp.float32)
    keyval_term = contract_first(normed, d_keyval_low)
    gain_terms = jnp.stack([gain_input, gain_post_attn, gain_pre_mlp, gain_post_mlp])
    head_terms = jnp.stack([gain_query_all, gain_key])
    gain_grad, head_grad, keyval_weight_grad = (
        lax.psum_scatter(
            gain_terms.astype(jnp.bfloat16), ("fsdp", "context"), scatter_dimension=1, tiled=True
        ).astype(jnp.float32),
        lax.psum_scatter(
            head_terms.astype(jnp.bfloat16), ("fsdp", "context"), scatter_dimension=1, tiled=True
        ).astype(jnp.float32),
        lax.psum_scatter(
            keyval_term.astype(jnp.bfloat16), ("fsdp", "context"), scatter_dimension=0, tiled=True
        ).astype(jnp.float32),
    )
    return (
        result[None].astype(jnp.bfloat16),
        input_total[None].astype(jnp.bfloat16),
        gain_grad,
        head_grad,
        attn_grads[:, 0],
        keyval_weight_grad,
        attn_grads[:, 1],
        jnp.stack([gate_grad, up_grad], axis=1),
        down_grad,
    )


def solution(mesh):
    return jax.shard_map(
        shards,
        mesh=mesh,
        in_specs=(
            P("fsdp", "context", None),
            P("fsdp", "context"),
            P("fsdp", "context"),
            P(None, ("fsdp", "context")),
            P(None, ("fsdp", "context")),
            P(("fsdp", "context"), "tensor"),
            P(("fsdp", "context"), None),
            P(("fsdp", "context"), "tensor"),
            P(("fsdp", "context"), None, "tensor"),
            P(("fsdp", "context"), "tensor"),
            P("fsdp", "context", None),
        ),
        out_specs=(
            P("fsdp", "context", None),
            P("fsdp", "context", None),
            P(None, ("fsdp", "context")),
            P(None, ("fsdp", "context")),
            P(("fsdp", "context"), "tensor"),
            P(("fsdp", "context"), None),
            P(("fsdp", "context"), "tensor"),
            P(("fsdp", "context"), None, "tensor"),
            P(("fsdp", "context"), "tensor"),
        ),
        check_vma=False,
    )
```

profile of v0, /device:TPU:0, one launch (start us, length us, event | category | flops | bytes accessed | tf_op | source)
XLA Modules:
  0.0 1111.7 jit_solution(1959116816128827641)
XLA Ops:
  14.3 18.8 %all-gather.1 = bf16[8,32,2]{1,2,0:T(2,128)(2,1)S(1)} all-gather(bf16[1,32,2]{1,2,0:T(2,128)(2,1)} %bitcast.266), channel_id=1, replica_groups=mesh['fsdp'=2,'context'=4,'tensor'=4] {'fsdp','context'}, dimensions={0}, use_global_device_ids=true | all-gather | bytes 1152 | tf_op jit(solution)/shard_map/all_gather | solution.py:73
  33.2 27.2 %all-gather = bf16[8,144,4]{1,2,0:T(4,128)(2,1)S(1)} all-gather(bf16[1,144,4]{1,2,0:T(4,128)(2,1)} %bitcast.265), channel_id=1, replica_groups=mesh['fsdp'=2,'context'=4,'tensor'=4] {'fsdp','context'}, dimensions={0}, use_global_device_ids=true | all-gather | bytes 10368 | tf_op jit(solution)/shard_map/all_gather | solution.py:72
  62.8 32.5 %all_gather.26 = bf16[1152,256]{1,0:T(8,128)(2,1)S(1)} all-gather(bf16[144,256]{1,0:T(8,128)(2,1)} %param.20), channel_id=1, replica_groups=mesh['fsdp'=2,'context'=4,'tensor'=4] {'fsdp','context'}, dimensions={0}, use_global_device_ids=true | all-gather | bytes 663552 | tf_op jit(solution)/shard_map/all_gather | solution.py:74
  104.4 33.8 %all_gather.27 = bf16[1152,256]{1,0:T(8,128)(2,1)S(1)} all-gather(bf16[144,256]{1,0:T(8,128)(2,1)S(1)} %copy-done.32), channel_id=1, replica_groups=mesh['fsdp'=2,'context'=4,'tensor'=4] {'fsdp','context'}, dimensions={0}, use_global_device_ids=true | all-gather | bytes 663552 | tf_op jit(solution)/shard_map/all_gather | solution.py:76
  146.2 36.1 %all-reduce.13.cloned.1.call-done = bf16[512,1152]{1,0:T(8,128)(2,1)} async-done(((bf16[512,1152]{1,0:T(8,128)(2,1)}), bf16[512,1152]{1,0:T(8,128)(2,1)}) %all-reduce.13.cloned.1.call-update) | async-done | bytes 1179664 | tf_op jit(solution)/shard_map/psum | solution.py:136
  188.6 119.4 %all-gather.8.cloned.1.call-done = bf16[1152,2,1728]{2,0,1:T(8,128)(2,1)} async-done(((bf16[144,2,1728]{2,0,1:T(8,128)(2,1)}), bf16[1152,2,1728]{2,0,1:T(8,128)(2,1)}) %all-gather.8.cloned.1.call-update) | async-done | bytes 7962640 | tf_op jit(solution)/shard_map/all_gather | solution.py:147
  308.0 8.2 fusion.114
  321.5 58.5 %all-gather.10.cloned.1.call-done = bf16[1152,1728]{1,0:T(8,128)(2,1)} async-done(((bf16[144,1728]{1,0:T(8,128)(2,1)}), bf16[1152,1728]{1,0:T(8,128)(2,1)}) %all-gather.10.cloned.1.call-update) | async-done | bytes 3981328 | tf_op jit(solution)/shard_map/all_gather | solution.py:154
  386.6 36.0 %all-reduce.15.cloned.1.call-done = bf16[512,1152]{1,0:T(8,128)(2,1)} async-done(((bf16[512,1152]{1,0:T(8,128)(2,1)}), bf16[512,1152]{1,0:T(8,128)(2,1)}) %all-reduce.15.cloned.1.call-update) | async-done | bytes 1179664 | tf_op jit(solution)/shard_map/psum | solution.py:152
  427.9 10.7 multiply_bitcast_fusion
  440.3 8.1 fusion.7
  450.2 36.1 %all-reduce.17.cloned.1.call-done = bf16[512,1152]{1,0:T(8,128)(2,1)} async-done(((bf16[512,1152]{1,0:T(8,128)(2,1)}), bf16[512,1152]{1,0:T(8,128)(2,1)}) %all-reduce.17.cloned.1.call-update) | async-done | bytes 1179664 | tf_op jit(solution)/shard_map/psum | solution.py:176
  505.7 11.6 %collective-permute-done.2 = bf16[512,512]{0,1:T(8,128)(2,1)S(1)} collective-permute-done((bf16[512,512]{0,1:T(8,128)(2,1)S(1)}, bf16[512,512]{0,1:T(8,128)(2,1)S(1)}, u32[]{:S(2)}, u32[]{:S(2)}) %collective-permute-start.2) | collective-permute-done | bytes 524320 | tf_op jit(solution)/shard_map/ppermute | solution.py:14
  523.5 7.2 psum.47
  535.6 27.2 %all-reduce.19.cloned.1.call-done = (bf16[512,1152]{1,0:T(8,128)(2,1)}, bf16[512,512]{0,1:T(8,128)(2,1)}) async-done(((bf16[512,1152]{1,0:T(8,128)(2,1)}, bf16[512,512]{0,1:T(8,128)(2,1)}), (bf16[512,1152]{1,0:T(8,128)(2,1)}, bf16[512,512]{0,1:T(8,128)(2,1)})) %all-reduce.19.cloned.1.call-update) | async-done | bytes 1703952 | tf_op jit(solution)/shard_map/psum | solution.py:237
  579.3 9.3 convolution_convert_fusion
  598.6 6.5 copy.40
  617.8 16.4 %reduce-scatter.24.cloned.1.call-done = bf16[32,2]{1,0:T(8,128)(2,1)} async-done(((bf16[256,2]{1,0:T(8,128)(2,1)}), bf16[32,2]{1,0:T(8,128)(2,1)}) %reduce-scatter.24.cloned.1.call-update) | async-done | bytes 144
  635.6 60.7 %reduce-scatter.22.cloned.1.call-done = bf16[144,4]{1,0:T(8,128)(2,1)} async-done(((bf16[1152,4]{1,0:T(8,128)(2,1)}), bf16[144,4]{1,0:T(8,128)(2,1)}) %reduce-scatter.22.cloned.1.call-update) | async-done | bytes 1168
  697.8 65.6 %reduce-scatter.16.cloned.1.call-done = bf16[144,2,256]{2,0,1:T(8,128)(2,1)} async-done(((bf16[1152,2,256]{2,0,1:T(8,128)(2,1)}), bf16[144,2,256]{2,0,1:T(8,128)(2,1)}) %reduce-scatter.16.cloned.1.call-update) | async-done | bytes 147472 | tf_op jit(solution)/shard_map/reduce_scatter | solution.py:252
  765.0 65.4 %reduce-scatter.18.cloned.1.call-done = bf16[144,512]{1,0:T(8,128)(2,1)} async-done(((bf16[1152,512]{1,0:T(8,128)(2,1)}), bf16[144,512]{1,0:T(8,128)(2,1)}) %reduce-scatter.18.cloned.1.call-update) | async-done | bytes 147472 | tf_op jit(solution)/shard_map/reduce_scatter | solution.py:270
  832.1 88.7 %reduce-scatter.26.cloned.1.call-done = bf16[144,1728]{1,0:T(8,128)(2,1)} async-done(((bf16[1152,1728]{1,0:T(8,128)(2,1)}), bf16[144,1728]{1,0:T(8,128)(2,1)}) %reduce-scatter.26.cloned.1.call-update) | async-done | bytes 497680
  923.1 88.9 %reduce-scatter.28.cloned.1.call-done = bf16[144,1728]{1,0:T(8,128)(2,1)} async-done(((bf16[1152,1728]{1,0:T(8,128)(2,1)}), bf16[144,1728]{1,0:T(8,128)(2,1)}) %reduce-scatter.28.cloned.1.call-update) | async-done | bytes 497680
  1019.2 83.7 %reduce-scatter.20.cloned.1.call-done = bf16[144,1728]{1,0:T(8,128)(2,1)} async-done(((bf16[1152,1728]{1,0:T(8,128)(2,1)}), bf16[144,1728]{1,0:T(8,128)(2,1)}) %reduce-scatter.20.cloned.1.call-update) | async-done | bytes 497680 | tf_op jit(solution)/shard_map/reduce_scatter | solution.py:185
  (303 shorter events, 139.8 us)
Async XLA Ops:
  7.2 91.9 %all-gather.6.cloned.1.call-start = ((), (), s32[]{:S(2)}) async-start(), calls=%async_computation.7 | async-start | bytes 1327104 | tf_op jit(solution)/shard_map/all_gather | solution.py:75
  7.9 174.4 %all-reduce.13.cloned.1.call-start = ((), (), s32[]{:S(2)}) async-start(), calls=%async_computation.8 | async-start | bytes 2359296 | tf_op jit(solution)/shard_map/psum | solution.py:136
  8.7 129.6 %collective-permute-start.1 = (s32[2,512]{1,0:T(2,128)S(1)}, s32[2,512]{1,0:T(2,128)S(1)}, u32[]{:S(2)}, u32[]{:S(2)}) collective-permute-start(s32[2,512]{1,0:T(2,128)S(1)} %pad_add_fusion.2), channel_id=1, source_target_pairs={{0,4},{4,8},{8,12},{1,5},{5,9},{9,13},{2,6},{6,10},{10,14},{3,7},{... | collective-permute-start | bytes 12296 | tf_op jit(solution)/shard_map/ppermute | solution.py:14
  14.3 87.4 %copy-start.37 = (f32[512]{0:T(512)}, f32[512]{0:T(512)S(1)}, u32[]{:S(2)}) copy-start(f32[512]{0:T(512)S(1)} %convert_element_type.178) | copy-start | bytes 6148
  60.5 41.2 %copy-start.73 = (f32[128]{0:T(128)}, f32[128]{0:T(128)S(1)}, u32[]{:S(2)}) copy-start(f32[128]{0:T(128)S(1)} %multiply_power_fusion) | copy-start | bytes 1540
  61.1 38.0 %copy-start.44 = (f32[1152]{0:T(1024)}, f32[1152]{0:T(1024)S(1)}, u32[]{:S(2)}) copy-start(f32[1152]{0:T(1024)S(1)} %get-tuple-element.146) | copy-start | bytes 13828
  62.8 38.8 %copy-start.61 = (f32[1,256]{1,0:T(1,128)}, f32[1,256]{1,0:T(1,128)S(1)}, u32[]{:S(2)}) copy-start(f32[1,256]{1,0:T(1,128)S(1)} %get-tuple-element.172) | copy-start | bytes 3076
  101.5 36.7 %copy-start.60 = (s32[1,512]{1,0:T(1,128)S(1)}, s32[1,512]{1,0:T(1,128)}, u32[]{:S(2)}) copy-start(s32[1,512]{1,0:T(1,128)} %param.16) | copy-start | bytes 6148
  101.6 36.7 %copy-start.67 = (s32[1,512]{1,0:T(1,128)S(1)}, s32[1,512]{1,0:T(1,128)}, u32[]{:S(2)}) copy-start(s32[1,512]{1,0:T(1,128)} %param.17) | copy-start | bytes 6148
  103.0 35.3 %collective-permute-start = (bf16[512,512]{0,1:T(8,128)(2,1)S(1)}, bf16[512,512]{0,1:T(8,128)(2,1)S(1)}, u32[]{:S(2)}, u32[]{:S(2)}) collective-permute-start(bf16[512,512]{0,1:T(8,128)(2,1)S(1)} %pad_maximum_fusion.2), channel_id=1, source_target_pairs={{0,4},{4,8},{8,12},{1,5},{5,9},{9,13},{2,6},{6,10},{10,14},{3,7},{... | collective-permute-start | bytes 1572872 | tf_op jit(solution)/shard_map/ppermute | solution.py:14
  143.0 165.0 %all-gather.8.cloned.1.call-start = ((), (), s32[]{:S(2)}) async-start(), calls=%async_computation.9 | async-start | bytes 9289728 | tf_op jit(solution)/shard_map/all_gather | solution.py:147
  145.4 234.7 %all-gather.10.cloned.1.call-start = ((), (), s32[]{:S(2)}) async-start(), calls=%async_computation.10 | async-start | bytes 4644864 | tf_op jit(solution)/shard_map/all_gather | solution.py:154
  145.9 276.7 %all-reduce.15.cloned.1.call-start = ((), (), s32[]{:S(2)}) async-start(), calls=%async_computation.11 | async-start | bytes 2359296 | tf_op jit(solution)/shard_map/psum | solution.py:152
  182.3 125.7 %copy-start = (bf16[512,1152]{1,0:T(8,128)(2,1)S(1)}, bf16[512,1152]{1,0:T(8,128)(2,1)}, u32[]{:S(2)}) copy-start(bf16[512,1152]{1,0:T(8,128)(2,1)} %all-reduce.13.cloned.1.call-done) | copy-start | bytes 3538948
  386.4 100.0 %all-reduce.17.cloned.1.call-start = ((), (), s32[]{:S(2)}) async-start(), calls=%async_computation.12 | async-start | bytes 2359296 | tf_op jit(solution)/shard_map/psum | solution.py:176
  448.5 114.3 %all-reduce.19.cloned.1.call-start = ((), (), s32[]{:S(2)}) async-start(), calls=%async_computation.20 | async-start | bytes 3407872 | tf_op jit(solution)/shard_map/psum | solution.py:237
  501.8 15.5 %collective-permute-start.2 = (bf16[512,512]{0,1:T(8,128)(2,1)S(1)}, bf16[512,512]{0,1:T(8,128)(2,1)S(1)}, u32[]{:S(2)}, u32[]{:S(2)}) collective-permute-start(bf16[512,512]{0,1:T(8,128)(2,1)S(1)} %fusion.66), channel_id=1, source_target_pairs={{4,0},{8,4},{12,8},{5,1},{9,5},{13,9},{6,2},{10,6},{14,10},{7,3},{... | collective-permute-start | bytes 1572872 | tf_op jit(solution)/shard_map/ppermute | solution.py:14
  518.3 115.9 %reduce-scatter.24.cloned.1.call-start = ((), (), s32[]{:S(2)}) async-start(), calls=%async_computation.17 | async-start | bytes 73728
  571.6 124.7 %reduce-scatter.22.cloned.1.call-start = ((), (), s32[]{:S(2)}) async-start(), calls=%async_computation.16 | async-start | bytes 331776
  574.6 188.8 %reduce-scatter.16.cloned.1.call-start = ((), (), s32[]{:S(2)}) async-start(), calls=%async_computation.13 | async-start | bytes 1327104 | tf_op jit(solution)/shard_map/reduce_scatter | solution.py:252
  575.9 254.5 %reduce-scatter.18.cloned.1.call-start = ((), (), s32[]{:S(2)}) async-start(), calls=%async_computation.14 | async-start | bytes 1327104 | tf_op jit(solution)/shard_map/reduce_scatter | solution.py:270
  579.2 341.6 %reduce-scatter.26.cloned.1.call-start = ((), (), s32[]{:S(2)}) async-start(), calls=%async_computation.18 | async-start | bytes 4644864
  598.6 413.3 %reduce-scatter.28.cloned.1.call-start = ((), (), s32[]{:S(2)}) async-start(), calls=%async_computation.19 | async-start | bytes 4644864
  605.2 497.7 %reduce-scatter.20.cloned.1.call-start = ((), (), s32[]{:S(2)}) async-start(), calls=%async_computation.15 | async-start | bytes 4644864 | tf_op jit(solution)/shard_map/reduce_scatter | solution.py:185
  (78 other events, 600.8 us)
Sparse Core Ops, SparseCore 0:
  10.1 43.7 all-gather.5
  143.1 39.0 all-reduce.12
  185.0 122.9 all-gather.7
  310.0 70.0 all-gather.9
  386.5 36.1 all-reduce.14
  448.6 37.7 all-reduce.16
  518.4 44.2 all-reduce.18
  571.7 62.4 reduce-scatter.23
  638.1 58.1 reduce-scatter.21
  699.5 63.8 reduce-scatter.15
  766.8 63.5 reduce-scatter.17
  833.8 86.9 reduce-scatter.25
  924.4 87.5 reduce-scatter.27
  1015.3 87.5 reduce-scatter.19
where the time goes:
time: 1120 us; the launch traced here: 1110 us
  waiting for transfers between devices  796 us (71%)
  blocking collectives  120 us (11%)
  matrix products  72.4 us (6%)
  local copies, waits for them, and re-layouts  50.5 us (5%)
  other arithmetic  49.1 us (4%)
  between operations  15.3 us (1%)
    unnamed x18, waiting for transfers between devices  256 us
    all_gather x1, waiting for transfers between devices, shards(): lax.all_gather(w_gateup, ('fsdp', 'context'), axis=0, tiled=True)  119 us
    reduce_scatter x1, waiting for transfers between devices, shards(): lax.psum_scatter(part.astype(jnp.bfloat16), ('fsdp', 'context'), scatter_...  83.7 us
    reduce_scatter x1, waiting for transfers between devices, shards(): lax.psum_scatter(jnp.stack([contract_first(features, d_query_low), contra...  65.6 us
    reduce_scatter x1, waiting for transfers between devices, shards(): lax.psum_scatter(keyval_term.astype(jnp.bfloat16), ('fsdp', 'context'), s...  65.4 us
    all_gather x1, waiting for transfers between devices, shards(): lax.all_gather(w_down, ('fsdp', 'context'), axis=0, tiled=True)  58.5 us
    unnamed x180, local copies, waits for them, and re-layouts  39.6 us
    psum x1, waiting for transfers between devices, shards(): lax.psum(d_normed_part.astype(jnp.bfloat16), 'tensor').astype(jnp.float32)  36.1 us
  transfers between devices with their start and end apart: 17, of which 14 were waited for; matrix products, arithmetic and copies ran while one was open for 9% of the time, Pallas kernels for 0%

commit v1 on v0

--- a/solution.py
+++ b/solution.py
@@ -6,6 +6,22 @@
 HD = 256
 WINDOW = 512
 EPSILON = 1e-06
+
+
+def summed_both_ways(x, axis, dim, product):
+    size, index, rows = (lax.axis_size(axis), lax.axis_index(axis), x.shape[dim])
+    right = [(i, (i + 1) % size) for i in range(size)]
+    left = [(i, (i - 1) % size) for i in range(size)]
+    middle = size // 2
+    from_left = from_right = x
+    running = product(x, index * rows)
+    for step in range(1, middle + 1):
+        from_left = lax.ppermute(from_left, axis, right)
+        if step < size - middle:
+            from_right = lax.ppermute(from_right, axis, left)
+            running = running + product(from_right, (index + step) % size * rows)
+        running = running + product(from_left, (index - step) % size * rows)
+    return running
 
 
 def from_behind(block, axis, distance):
@@ -141,11 +157,16 @@
     normed_mlp_f, pre_mlp_back = jax.vjp(rms_norm, hidden, gains_f[2])
     normed_mlp = normed_mlp_f.astype(jnp.bfloat16)
     columns = normed_mlp
-    gate_up = jnp.einsum(
-        "bn,nkf->bkf",
-        columns,
-        lax.all_gather(w_gateup, ("fsdp", "context"), axis=0, tiled=True),
-        preferred_element_type=jnp.float32,
+    gate_up = summed_both_ways(
+        w_gateup,
+        ("fsdp", "context"),
+        0,
+        lambda own_block, at: jnp.einsum(
+            "bn,nkf->bkf",
+            lax.dynamic_slice_in_dim(columns, at, own_block.shape[0], axis=1),
+            own_block,
+            preferred_element_type=jnp.float32,
+        ),
     )
     active_f, glu_back = jax.vjp(glu, gate_up)
     active = active_f.astype(jnp.bfloat16)

time: 1120 us -> 1190 us (1.062)
  blocking collectives: 120 us -> 182 us
  matrix products: 72.4 us -> 126 us
  waiting for transfers between devices: 796 us -> 746 us
  starting transfers between devices: 9.23 us -> 23.6 us
    all_gather x1, waiting for transfers between devices: 58.5 us -> 6.79 us  [shards(): lax.all_gather(w_down, ('fsdp', 'context'), axis=0, tiled=True)]
    all_gather x1, blocking collectives: 27.2 us -> 76.2 us  [shards(): lax.all_gather(norm_gains, ('fsdp', 'context'), axis=1, tiled=True)]
    dot_general x1 -> x8, matrix products: 8.16 us -> 57 us  [shards(): jnp.einsum('bn,nkf->bkf', lax.dynamic_slice_in_dim(columns, at, own_block...]
    unnamed x18, waiting for transfers between devices: 256 us -> 289 us
    ppermute x0 -> x7, waiting for transfers between devices: none -> 32.5 us  [the longest x3 32.5 us: summed_both_ways(): from_right = lax.ppermute(from_right, axis, left)]
    psum x1, waiting for transfers between devices: 27.2 us -> 7.78 us  [shards(): lax.psum(contract_last(d_query_low, query_all).astype(jnp.bfloat16), 'ten...]
    psum x1, waiting for transfers between devices: 36.1 us -> 18.7 us  [shards(): lax.psum(contract_last(mixed_low, out_all).astype(jnp.bfloat16), 'tensor')]
    ppermute x0 -> x7, starting transfers between devices: none -> 16.1 us  [the longest x3 9.85 us: summed_both_ways(): from_right = lax.ppermute(from_right, axis, left)]
  transfers between devices with their start and end apart: 17 -> 24, of which waited for: 14 -> 15; matrix products, arithmetic and copies ran while one was open for 9% -> 15% of each run, Pallas kernels for 0% -> 0%
where the time goes in v1:
time: 1190 us
  waiting for transfers between devices  746 us (63%)
  blocking collectives  182 us (15%)
  matrix products  126 us (11%)
  other arithmetic  51 us (4%)
  local copies, waits for them, and re-layouts  41.7 us (4%)
  starting transfers between devices  23.6 us (2%)
  between operations  15.4 us (1%)
    unnamed x18, waiting for transfers between devices  289 us
    all_gather x1, waiting for transfers between devices, shards(): lax.all_gather(w_gateup, ('fsdp', 'context'), axis=0, tiled=True)  108 us
    reduce_scatter x1, waiting for transfers between devices, shards(): lax.psum_scatter(part.astype(jnp.bfloat16), ('fsdp', 'context'), scatter_...  82 us
    all_gather x1, blocking collectives, shards(): lax.all_gather(norm_gains, ('fsdp', 'context'), axis=1, tiled=True)  76.2 us
    reduce_scatter x1, waiting for transfers between devices, shards(): lax.psum_scatter(jnp.stack([contract_first(features, d_query_low), contra...  65.8 us
    reduce_scatter x1, waiting for transfers between devices, shards(): lax.psum_scatter(keyval_term.astype(jnp.bfloat16), ('fsdp', 'context'), s...  65.2 us
    dot_general x8, matrix products, shards(): jnp.einsum('bn,nkf->bkf', lax.dynamic_slice_in_dim(columns, at, own_block...  57 us
    all_gather x1, blocking collectives, shards(): lax.all_gather(w_out, ('fsdp', 'context'), axis=0, tiled=True)  48.1 us
  transfers between devices with their start and end apart: 24, of which 15 were waited for; matrix products, arithmetic and copies ran while one was open for 15% of the time, Pallas kernels for 0%

profile of v1, /device:TPU:0, one launch (start us, length us, event | category | flops | bytes accessed | tf_op | source)
XLA Modules:
  0.0 1185.0 jit_solution(4331570488017971483)
XLA Ops:
  18.0 76.2 %all-gather = bf16[8,144,4]{1,2,0:T(4,128)(2,1)S(1)} all-gather(bf16[1,144,4]{1,2,0:T(4,128)(2,1)} %bitcast.290), channel_id=1, replica_groups=mesh['fsdp'=2,'context'=4,'tensor'=4] {'fsdp','context'}, dimensions={0}, use_global_device_ids=true | all-gather | bytes 10368 | tf_op jit(solution)/shard_map/all_gather | solution.py:88
  94.3 18.4 %all-gather.1 = bf16[8,32,2]{1,2,0:T(2,128)(2,1)S(1)} all-gather(bf16[1,32,2]{1,2,0:T(2,128)(2,1)} %bitcast.291), channel_id=1, replica_groups=mesh['fsdp'=2,'context'=4,'tensor'=4] {'fsdp','context'}, dimensions={0}, use_global_device_ids=true | all-gather | bytes 1152 | tf_op jit(solution)/shard_map/all_gather | solution.py:89
  114.3 32.9 %all_gather.25 = bf16[1152,256]{1,0:T(8,128)(2,1)S(1)} all-gather(bf16[144,256]{1,0:T(8,128)(2,1)S(1)} %copy-done.40), channel_id=1, replica_groups=mesh['fsdp'=2,'context'=4,'tensor'=4] {'fsdp','context'}, dimensions={0}, use_global_device_ids=true | all-gather | bytes 663552 | tf_op jit(solution)/shard_map/all_gather | solution.py:90
  161.9 48.1 %all_gather.26 = bf16[1152,256]{1,0:T(8,128)(2,1)S(1)} all-gather(bf16[144,256]{1,0:T(8,128)(2,1)S(1)} %copy-done.41), channel_id=1, replica_groups=mesh['fsdp'=2,'context'=4,'tensor'=4] {'fsdp','context'}, dimensions={0}, use_global_device_ids=true | all-gather | bytes 663552 | tf_op jit(solution)/shard_map/all_gather | solution.py:92
  223.4 32.5 %collective-permute-done.4 = bf16[144,2,1728]{2,0,1:T(8,128)(2,1)} collective-permute-done((bf16[144,2,1728]{2,0,1:T(8,128)(2,1)}, bf16[144,2,1728]{2,0,1:T(8,128)(2,1)}, u32[]{:S(2)}, u32[]{:S(2)}) %collective-permute-start.4) | collective-permute-done | bytes 995360 | tf_op jit(solution)/shard_map/ppermute | solution.py:21
  258.0 18.7 %all-reduce.13.cloned.1.call-done = bf16[512,1152]{1,0:T(8,128)(2,1)} async-done(((bf16[512,1152]{1,0:T(8,128)(2,1)}), bf16[512,1152]{1,0:T(8,128)(2,1)}) %all-reduce.13.cloned.1.call-update) | async-done | bytes 1179664 | tf_op jit(solution)/shard_map/psum | solution.py:152
  318.1 20.6 %add_add_fusion = f32[512,2,1728]{0,2,1:T(8,128)} fusion(f32[512,2,1728]{0,2,1:T(8,128)} %fusion.111, f32[512,2,1728]{0,2,1:T(8,128)} %fusion.113, f32[512,2,1728]{0,2,1:T(8,128)} %fusion.115, f32[512,2,1728]{0,2,1:T(8,128)} %fusion.117, f32[512,2,1728]{0,2,1:T(8,128)} %fusion.119, f32[512,2,1728]{0,2,1:T(8,128)} %fusion.123, f32[512,2,1728]{0,2,1:T(8,128)} %fusion.121, ...), kind=kOutput, calls=%fused_computation.3 | convolution fusion | flops 521994240 | bytes 57880580 | tf_op jit(solution)/shard_map/bn,nkf->bkf/dot_general | solution.py:164
  344.2 6.8 all-gather.8.cloned.1.call-done
  358.6 35.0 %all-reduce.15.cloned.1.call-done = bf16[512,1152]{1,0:T(8,128)(2,1)} async-done(((bf16[512,1152]{1,0:T(8,128)(2,1)}), bf16[512,1152]{1,0:T(8,128)(2,1)}) %all-reduce.15.cloned.1.call-update) | async-done | bytes 1179664 | tf_op jit(solution)/shard_map/psum | solution.py:173
  399.1 11.9 %multiply_bitcast_fusion = (f32[512,1,1728]{0,2,1:T(8,128)}, f32[512,1,1728]{0,2,1:T(8,128)}) fusion(f32[512,2,1728]{0,2,1:T(8,128)} %add_add_fusion, bf16[1152,1728]{1,0:T(8,128)(2,1)} %all-gather.8.cloned.1.call-done, bf16[512,1152]{1,0:T(8,128)(2,1)S(1)} %copy-done.6, bf16[1,512,1152]{2,1,0:T(8,128)(2,1)} %param.25, f32[512]{0:T(512)S(1)} %multiply_multiply_fusion.8, ...), kind=kOutput, calls=%fused_computation.25 | convolution fusion | flops 2062614528 | bytes 20505088 | tf_op jit(solution)/shard_map/dot_general | solution.py:185
  411.0 108.2 %all-gather.10.cloned.1.call-done = bf16[1152,2,1728]{2,0,1:T(8,128)(2,1)} async-done(((bf16[144,2,1728]{2,0,1:T(8,128)(2,1)}), bf16[1152,2,1728]{2,0,1:T(8,128)(2,1)}) %all-gather.10.cloned.1.call-update) | async-done | bytes 7962640 | tf_op jit(solution)/shard_map/all_gather | solution.py:194
  519.2 11.4 fusion.7
  531.1 11.4 convolution_convert_fusion
  542.6 23.9 %all-reduce.17.cloned.1.call-done = bf16[512,1152]{1,0:T(8,128)(2,1)} async-done(((bf16[512,1152]{1,0:T(8,128)(2,1)}), bf16[512,1152]{1,0:T(8,128)(2,1)}) %all-reduce.17.cloned.1.call-update) | async-done | bytes 1179664 | tf_op jit(solution)/shard_map/psum | solution.py:197
  585.2 10.2 collective-permute-done.9
  608.8 6.5 copy.100
  633.1 7.8 all-reduce.19.cloned.1.call-done
  654.7 77.6 %reduce-scatter.26.cloned.1.call-done = bf16[144,1728]{1,0:T(8,128)(2,1)} async-done(((bf16[1152,1728]{1,0:T(8,128)(2,1)}), bf16[144,1728]{1,0:T(8,128)(2,1)}) %reduce-scatter.26.cloned.1.call-update) | async-done | bytes 497680
  733.7 89.8 %reduce-scatter.28.cloned.1.call-done = bf16[144,1728]{1,0:T(8,128)(2,1)} async-done(((bf16[1152,1728]{1,0:T(8,128)(2,1)}), bf16[144,1728]{1,0:T(8,128)(2,1)}) %reduce-scatter.28.cloned.1.call-update) | async-done | bytes 497680
  832.4 82.0 %reduce-scatter.20.cloned.1.call-done = bf16[144,1728]{1,0:T(8,128)(2,1)} async-done(((bf16[1152,1728]{1,0:T(8,128)(2,1)}), bf16[144,1728]{1,0:T(8,128)(2,1)}) %reduce-scatter.20.cloned.1.call-update) | async-done | bytes 497680 | tf_op jit(solution)/shard_map/reduce_scatter | solution.py:206
  920.5 60.0 %reduce-scatter.24.cloned.1.call-done = bf16[32,2]{1,0:T(8,128)(2,1)} async-done(((bf16[256,2]{1,0:T(8,128)(2,1)}), bf16[32,2]{1,0:T(8,128)(2,1)}) %reduce-scatter.24.cloned.1.call-update) | async-done | bytes 144
  981.8 60.6 %reduce-scatter.22.cloned.1.call-done = bf16[144,4]{1,0:T(8,128)(2,1)} async-done(((bf16[1152,4]{1,0:T(8,128)(2,1)}), bf16[144,4]{1,0:T(8,128)(2,1)}) %reduce-scatter.22.cloned.1.call-update) | async-done | bytes 1168
  1043.9 65.8 %reduce-scatter.16.cloned.1.call-done = bf16[144,2,256]{2,0,1:T(8,128)(2,1)} async-done(((bf16[1152,2,256]{2,0,1:T(8,128)(2,1)}), bf16[144,2,256]{2,0,1:T(8,128)(2,1)}) %reduce-scatter.16.cloned.1.call-update) | async-done | bytes 147472 | tf_op jit(solution)/shard_map/reduce_scatter | solution.py:273
  1111.4 65.2 %reduce-scatter.18.cloned.1.call-done = bf16[144,512]{1,0:T(8,128)(2,1)} async-done(((bf16[1152,512]{1,0:T(8,128)(2,1)}), bf16[144,512]{1,0:T(8,128)(2,1)}) %reduce-scatter.18.cloned.1.call-update) | async-done | bytes 147472 | tf_op jit(solution)/shard_map/reduce_scatter | solution.py:291
  (326 shorter events, 188.2 us)
Async XLA Ops:
  7.2 146.6 %all-gather.6.cloned.1.call-start = ((), (), s32[]{:S(2)}) async-start(), calls=%async_computation.7 | async-start | bytes 1327104 | tf_op jit(solution)/shard_map/all_gather | solution.py:91
  8.7 202.9 %collective-permute-start.2 = (bf16[144,2,1728]{2,0,1:T(8,128)(2,1)S(1)}, bf16[144,2,1728]{2,0,1:T(8,128)(2,1)}, u32[]{:S(2)}, u32[]{:S(2)}) collective-permute-start(bf16[144,2,1728]{2,0,1:T(8,128)(2,1)S(1)} %copy.66), channel_id=1, source_target_pairs={{0,28},{4,0},{8,4},{12,8},{16,12},{20,16},{24,20},{28,24},{1,29},{... | collective-permute-start | bytes 2985992 | tf_op jit(solution)/shard_map/ppermute | solution.py:21
  14.7 135.0 %collective-permute-start.3 = (bf16[144,2,1728]{2,0,1:T(8,128)(2,1)S(1)}, bf16[144,2,1728]{2,0,1:T(8,128)(2,1)}, u32[]{:S(2)}, u32[]{:S(2)}) collective-permute-start(bf16[144,2,1728]{2,0,1:T(8,128)(2,1)S(1)} %copy.66), channel_id=1, source_target_pairs={{0,4},{4,8},{8,12},{12,16},{16,20},{20,24},{24,28},{28,0},{1,5},{5... | collective-permute-start | bytes 2985992 | tf_op jit(solution)/shard_map/ppermute | solution.py:19
  14.8 262.0 %all-reduce.13.cloned.1.call-start = ((), (), s32[]{:S(2)}) async-start(), calls=%async_computation.8 | async-start | bytes 2359296 | tf_op jit(solution)/shard_map/psum | solution.py:152
  16.1 193.9 %collective-permute-start.1 = (s32[2,512]{1,0:T(2,128)}, s32[2,512]{1,0:T(2,128)}, u32[]{:S(2)}, u32[]{:S(2)}) collective-permute-start(s32[2,512]{1,0:T(2,128)} %pad_add_fusion.2), channel_id=1, source_target_pairs={{0,4},{4,8},{8,12},{1,5},{5,9},{9,13},{2,6},{6,10},{10,14},{3,7},{... | collective-permute-start | bytes 12296 | tf_op jit(solution)/shard_map/ppermute | solution.py:30
  149.7 65.6 %collective-permute-start.5 = (bf16[144,2,1728]{2,0,1:T(8,128)(2,1)}, bf16[144,2,1728]{2,0,1:T(8,128)(2,1)}, u32[]{:S(2)}, u32[]{:S(2)}) collective-permute-start(bf16[144,2,1728]{2,0,1:T(8,128)(2,1)} %collective-permute-done.3), channel_id=1, source_target_pairs={{0,4},{4,8},{8,12},{12,16},{16,20},{20,24},{24,28},{28,0},{1,5},{5... | collective-permute-start | bytes 2985992 | tf_op jit(solution)/shard_map/ppermute | solution.py:19
  159.2 56.1 %collective-permute-start = (bf16[512,512]{0,1:T(8,128)(2,1)}, bf16[512,512]{0,1:T(8,128)(2,1)}, u32[]{:S(2)}, u32[]{:S(2)}) collective-permute-start(bf16[512,512]{0,1:T(8,128)(2,1)} %pad_maximum_fusion.2), channel_id=1, source_target_pairs={{0,4},{4,8},{8,12},{1,5},{5,9},{9,13},{2,6},{6,10},{10,14},{3,7},{... | collective-permute-start | bytes 1572872 | tf_op jit(solution)/shard_map/ppermute | solution.py:30
  211.5 44.3 %collective-permute-start.4 = (bf16[144,2,1728]{2,0,1:T(8,128)(2,1)}, bf16[144,2,1728]{2,0,1:T(8,128)(2,1)}, u32[]{:S(2)}, u32[]{:S(2)}) collective-permute-start(bf16[144,2,1728]{2,0,1:T(8,128)(2,1)} %collective-permute-done.2), channel_id=1, source_target_pairs={{0,28},{4,0},{8,4},{12,8},{16,12},{20,16},{24,20},{28,24},{1,29},{... | collective-permute-start | bytes 2985992 | tf_op jit(solution)/shard_map/ppermute | solution.py:21
  215.3 40.5 %collective-permute-start.7 = (bf16[144,2,1728]{2,0,1:T(8,128)(2,1)}, bf16[144,2,1728]{2,0,1:T(8,128)(2,1)}, u32[]{:S(2)}, u32[]{:S(2)}) collective-permute-start(bf16[144,2,1728]{2,0,1:T(8,128)(2,1)} %collective-permute-done.5), channel_id=1, source_target_pairs={{0,4},{4,8},{8,12},{12,16},{16,20},{20,24},{24,28},{28,0},{1,5},{5... | collective-permute-start | bytes 2985992 | tf_op jit(solution)/shard_map/ppermute | solution.py:19
  222.5 128.5 %all-gather.8.cloned.1.call-start = ((), (), s32[]{:S(2)}) async-start(), calls=%async_computation.9 | async-start | bytes 4644864 | tf_op jit(solution)/shard_map/all_gather | solution.py:175
  223.2 170.4 %all-reduce.15.cloned.1.call-start = ((), (), s32[]{:S(2)}) async-start(), calls=%async_computation.10 | async-start | bytes 2359296 | tf_op jit(solution)/shard_map/psum | solution.py:173
  255.8 56.8 %collective-permute-start.6 = (bf16[144,2,1728]{2,0,1:T(8,128)(2,1)}, bf16[144,2,1728]{2,0,1:T(8,128)(2,1)}, u32[]{:S(2)}, u32[]{:S(2)}) collective-permute-start(bf16[144,2,1728]{2,0,1:T(8,128)(2,1)} %collective-permute-done.4), channel_id=1, source_target_pairs={{0,28},{4,0},{8,4},{12,8},{16,12},{20,16},{24,20},{28,24},{1,29},{... | collective-permute-start | bytes 2985992 | tf_op jit(solution)/shard_map/ppermute | solution.py:21
  255.8 62.3 %collective-permute-start.8 = (bf16[144,2,1728]{2,0,1:T(8,128)(2,1)}, bf16[144,2,1728]{2,0,1:T(8,128)(2,1)}, u32[]{:S(2)}, u32[]{:S(2)}) collective-permute-start(bf16[144,2,1728]{2,0,1:T(8,128)(2,1)} %collective-permute-done.7), channel_id=1, source_target_pairs={{0,4},{4,8},{8,12},{12,16},{16,20},{20,24},{24,28},{28,0},{1,5},{5... | collective-permute-start | bytes 2985992 | tf_op jit(solution)/shard_map/ppermute | solution.py:19
  357.3 161.9 %all-gather.10.cloned.1.call-start = ((), (), s32[]{:S(2)}) async-start(), calls=%async_computation.11 | async-start | bytes 9289728 | tf_op jit(solution)/shard_map/all_gather | solution.py:194
  357.9 208.5 %all-reduce.17.cloned.1.call-start = ((), (), s32[]{:S(2)}) async-start(), calls=%async_computation.12 | async-start | bytes 2359296 | tf_op jit(solution)/shard_map/psum | solution.py:197
  530.6 110.3 %all-reduce.19.cloned.1.call-start = ((), (), s32[]{:S(2)}) async-start(), calls=%async_computation.20 | async-start | bytes 3407872 | tf_op jit(solution)/shard_map/psum | solution.py:258
  579.9 15.5 %collective-permute-start.9 = (bf16[512,512]{0,1:T(8,128)(2,1)S(1)}, bf16[512,512]{0,1:T(8,128)(2,1)S(1)}, u32[]{:S(2)}, u32[]{:S(2)}) collective-permute-start(bf16[512,512]{0,1:T(8,128)(2,1)S(1)} %fusion.66), channel_id=1, source_target_pairs={{4,0},{8,4},{12,8},{5,1},{9,5},{13,9},{6,2},{10,6},{14,10},{7,3},{... | collective-permute-start | bytes 1572872 | tf_op jit(solution)/shard_map/ppermute | solution.py:30
  596.4 135.9 %reduce-scatter.26.cloned.1.call-start = ((), (), s32[]{:S(2)}) async-start(), calls=%async_computation.18 | async-start | bytes 4644864
  608.7 214.7 %reduce-scatter.28.cloned.1.call-start = ((), (), s32[]{:S(2)}) async-start(), calls=%async_computation.19 | async-start | bytes 4644864
  615.3 299.1 %reduce-scatter.20.cloned.1.call-start = ((), (), s32[]{:S(2)}) async-start(), calls=%async_computation.15 | async-start | bytes 4644864 | tf_op jit(solution)/shard_map/reduce_scatter | solution.py:206
  622.9 357.5 %reduce-scatter.24.cloned.1.call-start = ((), (), s32[]{:S(2)}) async-start(), calls=%async_computation.17 | async-start | bytes 73728
  650.1 392.4 %reduce-scatter.22.cloned.1.call-start = ((), (), s32[]{:S(2)}) async-start(), calls=%async_computation.16 | async-start | bytes 331776
  651.1 458.6 %reduce-scatter.16.cloned.1.call-start = ((), (), s32[]{:S(2)}) async-start(), calls=%async_computation.13 | async-start | bytes 1327104 | tf_op jit(solution)/shard_map/reduce_scatter | solution.py:273
  652.3 524.3 %reduce-scatter.18.cloned.1.call-start = ((), (), s32[]{:S(2)}) async-start(), calls=%async_computation.14 | async-start | bytes 1327104 | tf_op jit(solution)/shard_map/reduce_scatter | solution.py:291
  (86 other events, 1286.5 us)
Sparse Core Ops, SparseCore 0:
  14.9 58.7 all-gather.5
  222.6 54.1 all-reduce.12
  278.8 72.0 all-gather.7
  357.4 36.1 all-reduce.14
  396.2 122.9 all-gather.9
  530.7 35.6 all-reduce.16
  596.5 44.2 all-reduce.18
  644.4 87.8 reduce-scatter.25
  735.9 87.5 reduce-scatter.27
  826.9 87.4 reduce-scatter.19
  918.4 62.0 reduce-scatter.23
  984.2 58.2 reduce-scatter.21
  1045.8 63.8 reduce-scatter.15
  1112.9 63.6 reduce-scatter.17
